TPU v7x, 32 devices: a whole 2x2x4 slice. The times are simulated.
32 devices in a mesh: tm: 8 (over z, y), space: 4 (over x, core).
Axes of the slice: x: 2, y: 2, z: 4, core: 2. Of those that a mesh axis runs over, the one named last changes fastest.
Arguments:
- states: float32 [8, 3, 256, 1024], P('tm', None, 'space'), may hold values from -3 to 3
- background: float32 [3, 256, 1024], P(None, 'space'), may hold values from -3 to 3
- obs_cells: int32 [8, 4, 1024], P('tm'), may hold values from 0 to 262143
- obs_values: float32 [8, 4, 1024], P('tm'), may hold values from -3 to 3
- land_mask: int32 [256, 1024], P('space'), may hold values 0 or 1
Outputs:
- gradient: float32 [8, 3, 256, 1024], P('tm', None, 'space')
- next_states: float32 [8, 3, 256, 1024], P('tm', None, 'space')
All inputs are finite; a program needn't handle non-finite values. No bound on the sum of `land_mask` on one device may be relied on, other than what follows from the above.
Results may differ from a plain program's by a relative error of at most 0.0003.
Values sent between devices are 32-bit elements; how exact they have to be, the bound alone decides.
A program may use at most 64 MiB of HBM per device.

v0:
```python
import functools

import jax
import jax.numpy as jnp
from jax import lax
from jax.experimental import pallas as pl
from jax.experimental.pallas import tpu as pltpu
from jax.sharding import PartitionSpec as P

NSTEP = 4
PAD = 8

advect = 0.25
gravity = 1.0
coriolis = 0.1
diffuse = 0.1
defect_weight = 2.0
obs_weight = 4.0
step_length = 0.1

KEEP = 1.0 - 4.0 * diffuse
HALF = advect / 2.0
HALF_G = advect * gravity / 2.0

MESH = pl.DeviceIdType.MESH


def kernel(
    n_tm,
    n_sp,
    states,
    background,
    cells,
    values,
    land,
    gradient,
    nexts,
    xt,
    yt,
    z0,
    prev_end,
    lam_a,
    lam_b,
    land_i,
    mask,
    dense_x,
    dense_y,
    cells_n,
    values_n,
    send,
    recv,
):
    rows, cols = states.shape[1], states.shape[2]
    tm, sp = lax.axis_index("tm"), lax.axis_index("space")
    wide = rows + 2 * PAD
    tiles = wide // PAD
    low, high = 2 * PAD, 2 * PAD + rows
    has_next, has_next2 = tm < n_tm - 1, tm < n_tm - 2
    has_prev, has_prev2 = tm > 0, tm > 1
    has_up, has_down = sp > 0, sp < n_sp - 1

    def span(t):
        return pl.ds(pl.multiple_of(t * PAD, PAD), PAD)

    for start in (0, PAD, high, high + PAD):
        blank = jnp.zeros((3, PAD, cols), jnp.float32)
        for ref in (xt.at[0], yt.at[0], z0):
            ref[:, start : start + PAD] = blank
        land_i[start : start + PAD] = jnp.zeros((PAD, cols), jnp.int32)

    barrier = pltpu.get_barrier_semaphore()
    near = (
        (has_up, (tm, sp - 1)),
        (has_down, (tm, sp + 1)),
        (has_prev, (tm - 1, sp)),
        (has_next, (tm + 1, sp)),
        (has_prev2, (tm - 2, sp)),
        (has_next2, (tm + 2, sp)),
    )
    for there, device in near:

        @pl.when(there)
        def _(device=device):
            pl.semaphore_signal(barrier, inc=1, device_id=device, device_id_type=MESH)

    pl.semaphore_wait(barrier, sum(there.astype(jnp.int32) for there, _ in near))

    def copy(index, src, dst, device):
        return pltpu.make_async_remote_copy(
            src_ref=src,
            dst_ref=dst,
            send_sem=send.at[index],
            recv_sem=recv.at[index],
            device_id=device,
            device_id_type=MESH,
        )

    started = []

    def start(index, src, dst, device, sends, receives):
        entry = copy(index, src, dst, device)

        @pl.when(sends)
        def _():
            entry.start()

        started.append((entry, sends))
        return entry, receives

    def arrive(*pairs):
        for entry, receives in pairs:

            @pl.when(receives)
            def _(entry=entry):
                entry.wait_recv()

    above, below = (tm, sp - 1), (tm, sp + 1)
    back, back2, ahead = (tm - 1, sp), (tm - 2, sp), (tm + 1, sp)
    yes_up, yes_down = has_up, has_down
    head, tail = pl.ds(0, PAD), pl.ds(rows - PAD, PAD)
    inner = pl.ds(PAD, rows - 2 * PAD)
    x0, y0 = xt.at[0], yt.at[0]
    top, bottom = pl.ds(PAD, PAD), pl.ds(high, PAD)
    y_head, y_tail = pl.ds(low, PAD), pl.ds(high - PAD, PAD)
    y_inner = pl.ds(low + PAD, rows - 2 * PAD)

    halo = [
        start(0, states.at[:, head], x0.at[:, bottom], above, yes_up, yes_down),
        start(1, states.at[:, tail], x0.at[:, top], below, yes_down, yes_up),
        start(2, land.at[head], land_i.at[bottom], above, yes_up, yes_down),
        start(3, land.at[tail], land_i.at[top], below, yes_down, yes_up),
    ]
    edges_y = [
        start(4, states.at[:, head], y0.at[:, y_head], back, has_prev, has_next),
        start(5, states.at[:, tail], y0.at[:, y_tail], back, has_prev, has_next),
    ]
    edges_z = [
        start(6, states.at[:, head], z0.at[:, y_head], back2, has_prev2, has_next2),
        start(7, states.at[:, tail], z0.at[:, y_tail], back2, has_prev2, has_next2),
    ]
    obs_next = [
        start(8, cells, cells_n, back, has_prev, has_next),
        start(9, values, values_n, back, has_prev, has_next),
    ]
    body_y = start(10, states.at[:, inner], y0.at[:, y_inner], back, has_prev, has_next)
    body_z = start(11, states.at[:, inner], z0.at[:, y_inner], back2, has_prev2, has_next2)

    first_row = sp * rows - PAD
    shift = cols.bit_length() - 1

    def densify(cells, values, dense):
        width = min(cols, 256)

        def one(s, carry):
            cell = cells[pl.ds(s, 1), :]
            value = values[pl.ds(s, 1), :]
            row = lax.shift_right_logical(cell, shift) - first_row
            col = lax.bitwise_and(cell, cols - 1)
            count = cell.shape[1]
            level = lax.broadcasted_iota(jnp.int32, (wide, count), 0)
            hit = level == row
            upper = value.astype(jnp.bfloat16).astype(jnp.float32)
            lower = value - upper
            picks = jnp.concatenate(
                [
                    jnp.where(hit, 1.0, 0.0),
                    jnp.where(hit, upper, 0.0),
                    jnp.where(hit, lower, 0.0),
                ],
                axis=0,
            ).astype(jnp.bfloat16)

            def part(c, carry):
                place = pl.multiple_of(c * width, width)
                column = lax.broadcasted_iota(jnp.int32, (width, count), 0) + place
                spread = jnp.where(column == col, 1.0, 0.0).astype(jnp.bfloat16)
                out = lax.dot_general(
                    picks, spread, (((1,), (1,)), ((), ())), preferred_element_type=jnp.float32
                )
                dense[s, 0, PAD : PAD + wide, pl.ds(place, width)] = obs_weight * out[:wide]
                dense[s, 1, PAD : PAD + wide, pl.ds(place, width)] = obs_weight * (
                    out[wide : 2 * wide] + out[2 * wide :]
                )
                return carry

            return lax.fori_loop(0, cols // width, part, carry)

        lax.fori_loop(0, NSTEP, one, 0)

    sub = lax.broadcasted_iota(jnp.int32, (PAD, cols), 0)
    is_first, is_last = sub == 0, sub == PAD - 1

    def valid(t):
        row = sub + (first_row + (t - 1) * PAD)
        return jnp.where((row >= 0) & (row < rows * n_sp), 1.0, 0.0)

    def around(ref, field, t):
        here = ref[field, span(t), :]
        before = ref[field, span(t - 1), :]
        after = ref[field, span(t + 1), :]
        up = pltpu.roll(jnp.where(is_last, before, here), 1, 0)
        down = pltpu.roll(jnp.where(is_first, after, here), PAD - 1, 0)
        left = pltpu.roll(here, 1, 1)
        right = pltpu.roll(here, cols - 1, 1)
        return here, up, down, left, right

    def forward(levels):
        def step(s, carry):
            src, dst = levels.at[s], levels.at[s + 1]

            def tile(t, carry):
                h, hu, hd, hl, hr = around(src, 0, t)
                u, uu, ud, ul, ur = around(src, 1, t)
                v, vu, vd, vl, vr = around(src, 2, t)
                m = mask[span(t), :]
                flux = (1.0 + hr) * ur - (1.0 + hl) * ul + (1.0 + hd) * vd - (1.0 + hu) * vu
                dst[0, span(t), :] = valid(t) * (
                    KEEP * h - HALF * flux + diffuse * ((hu + hd) + (hl + hr))
                )
                dst[1, span(t), :] = m * (
                    KEEP * u
                    - HALF_G * (hr - hl)
                    + coriolis * v
                    + diffuse * ((uu + ud) + (ul + ur))
                )
                dst[2, span(t), :] = m * (
                    KEEP * v
                    - HALF_G * (hd - hu)
                    - coriolis * u
                    + diffuse * ((vu + vd) + (vl + vr))
                )
                return carry

            return lax.fori_loop(1, tiles + 1, tile, carry)

        lax.fori_loop(0, NSTEP, step, 0)

    def begin(levels, following, there, dense, lam):
        def tile(t, carry):
            m = mask[span(t), :]
            ends = levels.at[NSTEP]

            def drive(field):
                defect = following[field, span(t), :] - ends[field, span(t), :]
                return jnp.where(there, -defect_weight * defect, 0.0)

            push = dense[NSTEP - 1, 0, span(t), :] * ends[0, span(t), :]
            push = push - dense[NSTEP - 1, 1, span(t), :]
            lam[0, span(t), :] = valid(t) * (drive(0) + push)
            lam[1, span(t), :] = m * drive(1)
            lam[2, span(t), :] = m * drive(2)
            return carry

        lax.fori_loop(1, tiles + 1, tile, 0)

    def adjoint_tile(src, state, t):
        p, pu, pd, pleft, pr = around(src, 0, t)
        q, qu, qd, ql, qr = around(src, 1, t)
        r, ru, rd, rl, rr = around(src, 2, t)
        depth = 1.0 + state[0, span(t), :]
        dx = HALF * (pr - pleft)
        dy = HALF * (pd - pu)
        lam_h = (
            KEEP * p
            + diffuse * ((pu + pd) + (pleft + pr))
            + state[1, span(t), :] * dx
            + state[2, span(t), :] * dy
            + HALF_G * ((qr - ql) + (rd - ru))
        )
        lam_u = KEEP * q + diffuse * ((qu + qd) + (ql + qr)) + depth * dx - coriolis * r
        lam_v = KEEP * r + diffuse * ((ru + rd) + (rl + rr)) + depth * dy + coriolis * q
        return lam_h, lam_u, lam_v

    def adjoint(levels, dense):
        src, dst = lam_a, lam_b
        for s in reversed(range(1, NSTEP)):

            def tile(t, carry, src=src, dst=dst, s=s):
                lam_h, lam_u, lam_v = adjoint_tile(src, levels.at[s], t)
                push = dense[s - 1, 0, span(t), :] * levels[s, 0, span(t), :]
                push = push - dense[s - 1, 1, span(t), :]
                m = mask[span(t), :]
                dst[0, span(t), :] = valid(t) * (lam_h + push)
                dst[1, span(t), :] = m * lam_u
                dst[2, span(t), :] = m * lam_v
                return carry

            lax.fori_loop(1, tiles + 1, tile, 0)
            src, dst = dst, src
        return src

    def place(t, carry):
        x0[:, span(t + 2), :] = states[:, span(t), :]
        land_i[span(t + 2), :] = land[span(t), :]
        return carry

    lax.fori_loop(0, rows // PAD, place, 0)
    densify(cells, values, dense_x)
    arrive(*halo)

    def to_mask(t, carry):
        mask[span(t), :] = land_i[span(t), :].astype(jnp.float32)
        return carry

    lax.fori_loop(0, tiles + 2, to_mask, 0)
    forward(xt)
    ends = start(
        12, xt.at[NSTEP, :, pl.ds(low, rows)], prev_end, ahead, has_next, has_prev
    )

    arrive(*edges_y)
    next_up = has_next & has_up
    next_down = has_next & has_down
    halo_y = [
        start(13, y0.at[:, y_head], y0.at[:, bottom], above, next_up, next_down),
        start(14, y0.at[:, y_tail], y0.at[:, top], below, next_down, next_up),
    ]
    arrive(*edges_z)
    next2_up = has_next2 & has_up
    next2_down = has_next2 & has_down
    halo_z = [
        start(15, z0.at[:, y_head], z0.at[:, bottom], above, next2_up, next2_down),
        start(16, z0.at[:, y_tail], z0.at[:, top], below, next2_down, next2_up),
    ]
    arrive(*obs_next)
    densify(cells_n, values_n, dense_y)
    arrive(body_y, *halo_y)

    begin(xt, y0, has_next, dense_x, lam_a)
    last = adjoint(xt, dense_x)

    def own(t, carry):
        lam = adjoint_tile(last, x0, t)
        for field in range(3):
            gradient[field, span(t - 2), :] = lam[field]
        return carry

    lax.fori_loop(2, tiles, own, 0)

    forward(yt)
    arrive(body_z, *halo_z)
    begin(yt, z0, has_next2, dense_y, lam_a)
    last = adjoint(yt, dense_y)

    def other(t, carry):
        lam = adjoint_tile(last, y0, t)
        for field in range(3):
            state = y0[field, span(t), :]
            end = xt[NSTEP, field, span(t), :]
            grad = defect_weight * (state - end) + lam[field]
            nexts[field, span(t - 2), :] = jnp.where(has_next, state - step_length * grad, end)
        return carry

    lax.fori_loop(2, tiles, other, 0)

    arrive(ends)

    def finish(t, carry):
        for field in range(3):
            before = jnp.where(
                has_prev, prev_end[field, span(t), :], background[field, span(t), :]
            )
            defect = states[field, span(t), :] - before
            gradient[field, span(t), :] = gradient[field, span(t), :] + defect_weight * defect
        return carry

    lax.fori_loop(0, rows // PAD, finish, 0)

    for entry, sends in started:

        @pl.when(sends)
        def _(entry=entry):
            entry.wait_send()


def solution(mesh):
    n_tm, n_sp = mesh.shape["tm"], mesh.shape["space"]

    def local(states, background, obs_cells, obs_values, land_mask):
        _, fields, rows, cols = states.shape
        padded = rows + 4 * PAD
        block = jax.ShapeDtypeStruct((fields, rows, cols), jnp.float32)
        f32 = functools.partial(pltpu.VMEM, dtype=jnp.float32)
        gradient, nexts = pl.pallas_call(
            functools.partial(kernel, n_tm, n_sp),
            out_shape=(block, block),
            in_specs=[pl.BlockSpec(memory_space=pltpu.VMEM)] * 5,
            out_specs=(pl.BlockSpec(memory_space=pltpu.VMEM),) * 2,
            scratch_shapes=[
                f32((NSTEP + 1, fields, padded, cols)),
                f32((NSTEP + 1, fields, padded, cols)),
                f32((fields, padded, cols)),
                f32((fields, rows, cols)),
                f32((fields, padded, cols)),
                f32((fields, padded, cols)),
                pltpu.VMEM((padded, cols), jnp.int32),
                f32((padded, cols)),
                f32((NSTEP, 2, padded, cols)),
                f32((NSTEP, 2, padded, cols)),
                pltpu.VMEM(obs_cells.shape[1:], jnp.int32),
                f32(obs_values.shape[1:]),
                pltpu.SemaphoreType.DMA((17,)),
                pltpu.SemaphoreType.DMA((17,)),
            ],
            compiler_params=pltpu.CompilerParams(
                collective_id=0, has_side_effects=True, vmem_limit_bytes=60 * 2**20
            ),
        )(states[0], background, obs_cells[0], obs_values[0], land_mask)
        return gradient[None], nexts[None]

    in_specs = (
        P("tm", None, "space", None),
        P(None, "space", None),
        P("tm", None, None),
        P("tm", None, None),
        P("space", None),
    )
    out_specs = (P("tm", None, "space", None), P("tm", None, "space", None))
    return jax.shard_map(local, mesh=mesh, in_specs=in_specs, out_specs=out_specs, check_vma=False)
```

profile of v0, /device:TPU:16, one launch (start us, length us, event | category | flops | bytes accessed | tf_op | source)
XLA Modules:
  0.0 60.9 jit_solution(10390088455366973143)
XLA Ops:
  0.6 57.2 %shard_map.68 = (f32[3,64,1024]{2,1,0:T(8,128)}, f32[3,64,1024]{2,1,0:T(8,128)}) custom-call(f32[3,64,1024]{2,1,0:T(8,128)} %bitcast.5, f32[3,64,1024]{2,1,0:T(8,128)} %background.1, s32[4,1024]{1,0:T(4,128)} %bitcast.8, f32[4,1024]{1,0:T(4,128)} %bitcast.9, s32[64,1024]{1,0:T(8,128)} %land.1), custom_call_target="tpu_custom_call" | custom-call | tf_op jit(solution)/shard_map/pallas_call | solution.py:384
  57.8 0.0 copy-start
  57.9 2.2 %copy.9 = f32[1,3,64,1024]{3,2,1,0:T(8,128)} copy(f32[1,3,64,1024]{3,2,1,0:T(8,128)} %bitcast.7) | data formatting | bytes 1572864
  60.0 0.0 copy-done
  60.0 0.9 %copy.10 = f32[1,3,64,1024]{3,2,1,0:T(8,128)} copy(f32[1,3,64,1024]{3,2,1,0:T(8,128)S(1)} %bitcast.6) | data formatting | bytes 1572864
Async XLA Ops:
  57.8 2.2 %copy-start = (f32[3,64,1024]{2,1,0:T(8,128)S(1)}, f32[3,64,1024]{2,1,0:T(8,128)}, u32[]{:S(2)}) copy-start(f32[3,64,1024]{2,1,0:T(8,128)} %get-tuple-element.5) | copy-start | bytes 2359300
where the time goes:
time: 61.1 us; the launch traced here: 60.9 us
  Pallas kernels  57.2 us (94%)
  local copies, waits for them, and re-layouts  3.04 us (5%)
  between operations  0.65 us (1%)
    pallas_call x1, Pallas kernels, local(): pl.pallas_call(functools.partial(kernel, n_tm, n_sp), out_shape=(block, b...  57.2 us
    unnamed x4, local copies, waits for them, and re-layouts  3.04 us

commit v1 on v0

--- a/solution.py
+++ b/solution.py
@@ -118,11 +118,9 @@
     back, back2, ahead = (tm - 1, sp), (tm - 2, sp), (tm + 1, sp)
     yes_up, yes_down = has_up, has_down
     head, tail = pl.ds(0, PAD), pl.ds(rows - PAD, PAD)
-    inner = pl.ds(PAD, rows - 2 * PAD)
     x0, y0 = xt.at[0], yt.at[0]
     top, bottom = pl.ds(PAD, PAD), pl.ds(high, PAD)
     y_head, y_tail = pl.ds(low, PAD), pl.ds(high - PAD, PAD)
-    y_inner = pl.ds(low + PAD, rows - 2 * PAD)
 
     halo = [
         start(0, states.at[:, head], x0.at[:, bottom], above, yes_up, yes_down),
@@ -130,25 +128,51 @@
         start(2, land.at[head], land_i.at[bottom], above, yes_up, yes_down),
         start(3, land.at[tail], land_i.at[top], below, yes_down, yes_up),
     ]
-    edges_y = [
-        start(4, states.at[:, head], y0.at[:, y_head], back, has_prev, has_next),
-        start(5, states.at[:, tail], y0.at[:, y_tail], back, has_prev, has_next),
-    ]
-    edges_z = [
-        start(6, states.at[:, head], z0.at[:, y_head], back2, has_prev2, has_next2),
-        start(7, states.at[:, tail], z0.at[:, y_tail], back2, has_prev2, has_next2),
-    ]
+    even = lax.rem(tm, 2) == 0
+    odd = jnp.logical_not(even)
     obs_next = [
-        start(8, cells, cells_n, back, has_prev, has_next),
-        start(9, values, values_n, back, has_prev, has_next),
-    ]
-    body_y = start(10, states.at[:, inner], y0.at[:, y_inner], back, has_prev, has_next)
-    body_z = start(11, states.at[:, inner], z0.at[:, y_inner], back2, has_prev2, has_next2)
+        start(4, cells, cells_n, back, has_prev, has_next),
+        start(5, values, values_n, back, has_prev, has_next),
+    ]
+    pieces = [0, rows - PAD, *range(PAD, rows - PAD, PAD)]
+    n_piece = len(pieces)
+    source = [pl.ds(row, PAD) for row in pieces]
+    target = [pl.ds(low + row, PAD) for row in pieces]
+    far = [
+        start(8 + i, states.at[:, source[i]], z0.at[:, target[i]], back2, has_prev2, has_next2)
+        for i in range(n_piece)
+    ]
+    direct = [
+        start(
+            8 + n_piece + i,
+            states.at[:, source[i]],
+            y0.at[:, target[i]],
+            back,
+            odd,
+            even & has_next,
+        )
+        for i in range(n_piece)
+    ]
+    relayed = []
+
+    def relay(count):
+        for i in range(len(relayed), min(len(relayed) + count, n_piece)):
+            arrive(far[i])
+            relayed.append(
+                start(
+                    8 + 2 * n_piece + i,
+                    z0.at[:, target[i]],
+                    y0.at[:, target[i]],
+                    ahead,
+                    even & has_next2,
+                    odd & has_next,
+                )
+            )
 
     first_row = sp * rows - PAD
     shift = cols.bit_length() - 1
 
-    def densify(cells, values, dense):
+    def densify(cells, values, dense, begin_at, end_at):
         width = min(cols, 256)
 
         def one(s, carry):
@@ -185,7 +209,7 @@
 
             return lax.fori_loop(0, cols // width, part, carry)
 
-        lax.fori_loop(0, NSTEP, one, 0)
+        lax.fori_loop(begin_at, end_at, one, 0)
 
     sub = lax.broadcasted_iota(jnp.int32, (PAD, cols), 0)
     is_first, is_last = sub == 0, sub == PAD - 1
@@ -295,7 +319,8 @@
         return carry
 
     lax.fori_loop(0, rows // PAD, place, 0)
-    densify(cells, values, dense_x)
+    half = NSTEP // 2
+    densify(cells, values, dense_x, 0, NSTEP)
     arrive(*halo)
 
     def to_mask(t, carry):
@@ -303,28 +328,34 @@
         return carry
 
     lax.fori_loop(0, tiles + 2, to_mask, 0)
+    relay(2)
     forward(xt)
-    ends = start(
-        12, xt.at[NSTEP, :, pl.ds(low, rows)], prev_end, ahead, has_next, has_prev
-    )
-
-    arrive(*edges_y)
+    relay(2)
+    arrive(*obs_next)
+    densify(cells_n, values_n, dense_y, 0, half)
+    relay(1)
+    densify(cells_n, values_n, dense_y, half, NSTEP)
+    relay(1)
+    arrive(*direct[:2], *relayed[:2])
     next_up = has_next & has_up
     next_down = has_next & has_down
-    halo_y = [
-        start(13, y0.at[:, y_head], y0.at[:, bottom], above, next_up, next_down),
-        start(14, y0.at[:, y_tail], y0.at[:, top], below, next_down, next_up),
-    ]
-    arrive(*edges_z)
     next2_up = has_next2 & has_up
     next2_down = has_next2 & has_down
-    halo_z = [
-        start(15, z0.at[:, y_head], z0.at[:, bottom], above, next2_up, next2_down),
-        start(16, z0.at[:, y_tail], z0.at[:, top], below, next2_down, next2_up),
-    ]
-    arrive(*obs_next)
-    densify(cells_n, values_n, dense_y)
-    arrive(body_y, *halo_y)
+    halo_next = [
+        start(6, y0.at[:, y_head], y0.at[:, bottom], above, next_up, next_down),
+        start(7, y0.at[:, y_tail], y0.at[:, top], below, next_down, next_up),
+    ]
+    base = 8 + 3 * n_piece
+    halo_far = [
+        start(base, z0.at[:, y_head], z0.at[:, bottom], above, next2_up, next2_down),
+        start(base + 1, z0.at[:, y_tail], z0.at[:, top], below, next2_down, next2_up),
+    ]
+    relay(n_piece)
+    arrive(*direct[2:], *relayed[2:])
+    ends = start(
+        base + 2, xt.at[NSTEP, :, pl.ds(low, rows)], prev_end, ahead, has_next, has_prev
+    )
+    arrive(*halo_next)
 
     begin(xt, y0, has_next, dense_x, lam_a)
     last = adjoint(xt, dense_x)
@@ -338,7 +369,7 @@
     lax.fori_loop(2, tiles, own, 0)
 
     forward(yt)
-    arrive(body_z, *halo_z)
+    arrive(*halo_far)
     begin(yt, z0, has_next2, dense_y, lam_a)
     last = adjoint(yt, dense_y)
 
@@ -399,8 +430,8 @@
                 f32((NSTEP, 2, padded, cols)),
                 pltpu.VMEM(obs_cells.shape[1:], jnp.int32),
                 f32(obs_values.shape[1:]),
-                pltpu.SemaphoreType.DMA((17,)),
-                pltpu.SemaphoreType.DMA((17,)),
+                pltpu.SemaphoreType.DMA((11 + 3 * (rows // PAD),)),
+                pltpu.SemaphoreType.DMA((11 + 3 * (rows // PAD),)),
             ],
             compiler_params=pltpu.CompilerParams(
                 collective_id=0, has_side_effects=True, vmem_limit_bytes=60 * 2**20

time: 61.1 us -> 53.1 us (0.87)
  Pallas kernels: 57.2 us -> 49 us
    pallas_call x1, Pallas kernels: 57.2 us -> 49 us  [local(): pl.pallas_call(functools.partial(kernel, n_tm, n_sp), out_shape=(block, b...]
where the time goes in v1:
time: 53.1 us; the launch traced here: 52.7 us
  Pallas kernels  49 us (92%)
  local copies, waits for them, and re-layouts  3.04 us (6%)
  between operations  0.65 us (1%)
    pallas_call x1, Pallas kernels, local(): pl.pallas_call(functools.partial(kernel, n_tm, n_sp), out_shape=(block, b...  49 us
    unnamed x4, local copies, waits for them, and re-layouts  3.04 us

profile of v1, /device:TPU:16, one launch (start us, length us, event | category | flops | bytes accessed | tf_op | source)
XLA Modules:
  0.0 52.7 jit_solution(3974656324195400886)
XLA Ops:
  0.6 49.0 %shard_map.68 = (f32[3,64,1024]{2,1,0:T(8,128)}, f32[3,64,1024]{2,1,0:T(8,128)}) custom-call(f32[3,64,1024]{2,1,0:T(8,128)} %bitcast.5, f32[3,64,1024]{2,1,0:T(8,128)} %background.1, s32[4,1024]{1,0:T(4,128)} %bitcast.8, f32[4,1024]{1,0:T(4,128)} %bitcast.9, s32[64,1024]{1,0:T(8,128)} %land.1), custom_call_target="tpu_custom_call" | custom-call | tf_op jit(solution)/shard_map/pallas_call | solution.py:415
  49.7 0.0 copy-start
  49.7 2.2 %copy.9 = f32[1,3,64,1024]{3,2,1,0:T(8,128)} copy(f32[1,3,64,1024]{3,2,1,0:T(8,128)} %bitcast.7) | data formatting | bytes 1572864
  51.8 0.0 copy-done
  51.8 0.9 %copy.10 = f32[1,3,64,1024]{3,2,1,0:T(8,128)} copy(f32[1,3,64,1024]{3,2,1,0:T(8,128)S(1)} %bitcast.6) | data formatting | bytes 1572864
Async XLA Ops:
  49.7 2.2 %copy-start = (f32[3,64,1024]{2,1,0:T(8,128)S(1)}, f32[3,64,1024]{2,1,0:T(8,128)}, u32[]{:S(2)}) copy-start(f32[3,64,1024]{2,1,0:T(8,128)} %get-tuple-element.5) | copy-start | bytes 2359300

commit v2 on v1

--- a/solution.py
+++ b/solution.py
@@ -351,11 +351,10 @@
         start(base + 1, z0.at[:, y_tail], z0.at[:, top], below, next2_down, next2_up),
     ]
     relay(n_piece)
-    arrive(*direct[2:], *relayed[2:])
     ends = start(
         base + 2, xt.at[NSTEP, :, pl.ds(low, rows)], prev_end, ahead, has_next, has_prev
     )
-    arrive(*halo_next)
+    arrive(*direct[2:], *relayed[2:], *halo_next)
 
     begin(xt, y0, has_next, dense_x, lam_a)
     last = adjoint(xt, dense_x)

time: 53.1 us -> 52.2 us (0.983)
  the two profiles are of different devices: /device:TPU:16 before, /device:TPU:0 now
where the time goes in v2:
time: 52.2 us; the launch traced here: 52 us
  Pallas kernels  48.3 us (93%)
  local copies, waits for them, and re-layouts  3.04 us (6%)
  between operations  0.65 us (1%)
    pallas_call x1, Pallas kernels, local(): pl.pallas_call(functools.partial(kernel, n_tm, n_sp), out_shape=(block, b...  48.3 us
    unnamed x4, local copies, waits for them, and re-layouts  3.04 us

profile of v2, /device:TPU:0, one launch (start us, length us, event | category | flops | bytes accessed | tf_op | source)
XLA Modules:
  0.0 52.0 jit_solution(15053806812472228050)
XLA Ops:
  0.6 48.3 %shard_map.68 = (f32[3,64,1024]{2,1,0:T(8,128)}, f32[3,64,1024]{2,1,0:T(8,128)}) custom-call(f32[3,64,1024]{2,1,0:T(8,128)} %bitcast.5, f32[3,64,1024]{2,1,0:T(8,128)} %background.1, s32[4,1024]{1,0:T(4,128)} %bitcast.8, f32[4,1024]{1,0:T(4,128)} %bitcast.9, s32[64,1024]{1,0:T(8,128)} %land.1), custom_call_target="tpu_custom_call" | custom-call | tf_op jit(solution)/shard_map/pallas_call | solution.py:414
  49.0 0.0 copy-start
  49.0 2.2 %copy.9 = f32[1,3,64,1024]{3,2,1,0:T(8,128)} copy(f32[1,3,64,1024]{3,2,1,0:T(8,128)} %bitcast.7) | data formatting | bytes 1572864
  51.1 0.0 copy-done
  51.1 0.9 %copy.10 = f32[1,3,64,1024]{3,2,1,0:T(8,128)} copy(f32[1,3,64,1024]{3,2,1,0:T(8,128)S(1)} %bitcast.6) | data formatting | bytes 1572864
Async XLA Ops:
  49.0 2.2 %copy-start = (f32[3,64,1024]{2,1,0:T(8,128)S(1)}, f32[3,64,1024]{2,1,0:T(8,128)}, u32[]{:S(2)}) copy-start(f32[3,64,1024]{2,1,0:T(8,128)} %get-tuple-element.5) | copy-start | bytes 2359300
